TPU v7x, 128 devices: a whole 4x4x4 slice. The times are simulated.
128 devices in a mesh: group: 8 (over y_hi, z), shard: 16 (over x, y_lo, core).
Axes of the slice: x: 4, y: 4 (y_hi: 2, y_lo: 2; y = y_hi * 2 + y_lo), z: 4, core: 2. Of those that a mesh axis runs over, the one named last changes fastest.
Arguments:
- hidden_state: bfloat16 [2048, 8192], P('group', 'shard'), may hold values from -40 to 40
- attn_gain: bfloat16 [8192], replicated, may hold values from 0.5 to 1.5
- ffn_gain: bfloat16 [8192], replicated, may hold values from 0.5 to 1.5
- w_query: bfloat16 [8192, 8192], P('group', 'shard'), may hold values from -0.125 to 0.125
- w_keyval: bfloat16 [8192, 2048], P('group', 'shard'), may hold values from -0.0625 to 0.0625
- w_output: bfloat16 [8192, 8192], P('shard', 'group'), may hold values from -0.0625 to 0.0625
- cache_keys: bfloat16 [2048, 8, 192, 128], P(('group', 'shard')), may hold values from -256 to 256
- cache_values: bfloat16 [2048, 8, 192, 128], P(('group', 'shard')), may hold values from -6 to 6
- lengths: int32 [2048], P('group'), may hold values from 2 to 192, as said below
Outputs:
- branch: bfloat16 [2048, 8192], P('group', 'shard')
- ffn_input: bfloat16 [2048, 8192], P('group', 'shard')
Inputs may be any that keep to these rules, and one draw needn't show every extreme that they name: `lengths`: in every aligned block of 16 sequences, at least one has all 192 cached positions live.
All inputs are finite; a program needn't handle non-finite values.
Results may differ from a plain program's by a relative error of at most 0.012.
The roundings to bfloat16 on the way count: a program that leaves them out, or rounds other values in their place, can miss the bound.
Values may be sent and summed in bfloat16 or wider, within the bound.
No kernel may reach another device: no remote copies, remote signals or barrier semaphores. Data moves between devices by JAX's collectives and lax.ppermute only.
A program may use at most 128 MiB of HBM per device.

v0:
```python
import jax
import jax.numpy as jnp
from jax import lax
from jax.sharding import PartitionSpec as P

epsilon = 1e-05
rope_base = 500000.0


def sent_together(arrays, axis, dim, along):
    both = jnp.concatenate(arrays, axis=along)
    filled, at, gathered = (lax.all_gather(both, axis, axis=dim, tiled=True), 0, [])
    for a in arrays:
        gathered.append(lax.slice_in_dim(filled, at, at + a.shape[along], axis=along))
        at += a.shape[along]
    return tuple(gathered)


def from_everyone(x, axis):
    devices = lax.axis_size(axis)
    return lax.all_to_all(jnp.broadcast_to(x[None], (devices, *x.shape)), axis, 0, 0, tiled=True)


def over_copies(x, axis):
    everything = from_everyone(x, axis)
    return jnp.sum(everything, axis=0)


def rotate(heads_block, position):
    head_dim = heads_block.shape[-1]
    half_dim = head_dim // 2
    frequency = rope_base ** (-2.0 * jnp.arange(half_dim, dtype=jnp.float32) / head_dim)
    angles = position.astype(jnp.float32)[:, None] * frequency[None, :]
    cosine = jnp.cos(angles)[:, None, :]
    sine_part = jnp.sin(angles)[:, None, :]
    lower_half = heads_block[..., :half_dim]
    upper_half = heads_block[..., half_dim:]
    return jnp.concatenate(
        [
            lower_half * cosine - upper_half * sine_part,
            upper_half * cosine + lower_half * sine_part,
        ],
        axis=-1,
    )


def attend(queries, fresh, cache_keys, cache_values, lengths):
    seq_count, kv_heads, cache_len, head_dim = cache_keys.shape
    q_heads = queries.shape[1] // head_dim
    q_per_kv = q_heads // kv_heads
    kv_width = kv_heads * head_dim
    grouped = queries.reshape(seq_count, kv_heads, q_per_kv, head_dim)
    new_keys = fresh[:, :kv_width].reshape(seq_count, kv_heads, head_dim)
    new_values = fresh[:, kv_width:].reshape(seq_count, kv_heads, head_dim)
    score_scale = head_dim ** (-0.5)
    scores = (
        jnp.einsum("nkgd,nkld->nkgl", grouped, cache_keys, preferred_element_type=jnp.float32)
        * score_scale
    )
    self_score = (
        jnp.einsum("nkgd,nkd->nkg", grouped, new_keys, preferred_element_type=jnp.float32)
        * score_scale
    )
    live_mask = jnp.arange(cache_len, dtype=jnp.int32)[None, :] < lengths[:, None]
    scores = jnp.where(live_mask[:, None, None, :], scores, -1e30)
    row_top = jnp.maximum(jnp.max(scores, axis=3), self_score)
    exp_scores = jnp.exp(scores - row_top[..., None])
    self_weight = jnp.exp(self_score - row_top)
    denom_sum = jnp.sum(exp_scores, axis=3) + self_weight
    weight_bf = (exp_scores / denom_sum[..., None]).astype(jnp.bfloat16)
    self_bf = (self_weight / denom_sum).astype(jnp.bfloat16)
    context = jnp.einsum(
        "nkgl,nkld->nkgd", weight_bf, cache_values, preferred_element_type=jnp.float32
    )
    context = (
        context
        + self_bf.astype(jnp.float32)[..., None] * new_values.astype(jnp.float32)[:, :, None, :]
    )
    return context.reshape(seq_count, q_heads * head_dim).astype(jnp.bfloat16)


def local(
    hidden_state,
    attn_gain,
    ffn_gain,
    w_query,
    w_keyval,
    w_output,
    cache_keys,
    cache_values,
    lengths,
):
    token_count, local_width = hidden_state.shape
    shard_count = lax.axis_size("shard")
    shard_pos = lax.axis_index("shard")
    model_width = local_width * shard_count
    col_start = shard_pos * local_width
    resident = hidden_state.astype(jnp.float32)
    attn_scale = attn_gain.astype(jnp.float32)
    whole_rows = lax.all_gather(hidden_state, "shard", axis=1, tiled=True).astype(jnp.float32)
    inverse = lax.rsqrt(jnp.mean(whole_rows * whole_rows, axis=1, keepdims=True) + epsilon)
    normed = (whole_rows * inverse * attn_scale).astype(jnp.bfloat16)
    pieces = sent_together((w_query, w_keyval), "group", 0, 1)
    queries = jnp.dot(normed, pieces[0], preferred_element_type=jnp.float32)
    keyval = jnp.dot(normed, pieces[1], preferred_element_type=jnp.float32)
    head_dim = cache_keys.shape[3]
    q_cols = queries.shape[1]
    kv_cols = keyval.shape[1]
    roped_q = (
        rotate(queries.reshape(token_count, q_cols // head_dim, head_dim), lengths)
        .reshape(token_count, q_cols)
        .astype(jnp.bfloat16)
    )
    turned = rotate(keyval.reshape(token_count, kv_cols // head_dim, head_dim), lengths).reshape(
        token_count, kv_cols
    )
    key_side = shard_pos * kv_cols < kv_cols * shard_count // 2
    fresh = jnp.where(key_side, turned, keyval).astype(jnp.bfloat16)
    owner_q, owner_kv = (
        lax.all_to_all(roped_q, "shard", split_axis=0, concat_axis=1, tiled=True),
        lax.all_to_all(fresh, "shard", split_axis=0, concat_axis=1, tiled=True),
    )
    seq_dev = cache_keys.shape[0]
    owner_len = lax.dynamic_slice_in_dim(lengths, shard_pos * seq_dev, seq_dev)
    context = attend(owner_q, owner_kv, cache_keys, cache_values, owner_len)
    back_rows = lax.all_to_all(context, "shard", split_axis=1, concat_axis=0, tiled=True)
    partial_value = jnp.dot(
        back_rows,
        lax.all_gather(w_output, "group", axis=1, tiled=True),
        preferred_element_type=jnp.float32,
    )
    summed = lax.psum_scatter(partial_value, "shard", scatter_dimension=1, tiled=True)
    ffn_scale = lax.dynamic_slice_in_dim(ffn_gain.astype(jnp.float32), col_start, local_width)
    stream = resident + summed
    branch = summed.astype(jnp.bfloat16)
    squares_two = over_copies(jnp.sum(stream * stream, axis=1), "shard")
    inverse_two = lax.rsqrt(squares_two / model_width + epsilon)[:, None]
    ffn_input = (stream * inverse_two * ffn_scale).astype(jnp.bfloat16)
    return (branch, ffn_input)


def solution(mesh):
    placed = (
        P("group", "shard"),
        P(),
        P(),
        P("group", "shard"),
        P("group", "shard"),
        P("shard", "group"),
        P(("group", "shard"), None, None, None),
        P(("group", "shard"), None, None, None),
        P("group"),
    )
    return jax.shard_map(
        local,
        mesh=mesh,
        in_specs=placed,
        out_specs=(P("group", "shard"), P("group", "shard")),
        check_vma=False,
    )
```

profile of v0, /device:TPU:1, one launch (start us, length us, event | category | flops | bytes accessed | tf_op | source)
XLA Modules:
  0.0 413.2 jit_solution(4423881980820156677)
XLA Ops:
  7.9 2.5 pad_maximum_fusion
  12.6 0.8 dynamic_slice.6
  14.0 36.4 %all-gather.4.cloned.1.call-done = bf16[256,8192]{1,0:T(8,128)(2,1)} async-done(((bf16[256,512]{1,0:T(8,128)(2,1)}), bf16[256,8192]{1,0:T(8,128)(2,1)}) %all-gather.4.cloned.1.call-update) | async-done | bytes 4194320 | tf_op jit(solution)/shard_map/all_gather | solution.py:100
  50.3 3.1 fusion
  53.5 123.9 %all-gather.6.cloned.1.call-done = bf16[8192,640]{1,0:T(8,128)(2,1)} async-done(((bf16[1024,640]{1,0:T(8,128)(2,1)}), bf16[8192,640]{1,0:T(8,128)(2,1)}) %all-gather.6.cloned.1.call-update) | async-done | bytes 10485776 | tf_op jit(solution)/shard_map/all_gather | solution.py:12
  177.4 4.6 %fusion.5 = f32[256,128]{0,1:T(8,128)S(1)} fusion(bf16[8192,640]{1,0:T(8,128)(2,1)} %all-gather.6.cloned.1.call-done, bf16[256,8192]{1,0:T(8,128)(2,1)} %all-gather.4.cloned.1.call-done, f32[8192]{0:T(1024)S(1)} %convert_element_type.60, f32[256]{0:T(256)S(1)} %add_rsqrt_fusion.1), kind=kOutput, calls=%fused_computation.7 | convolution fusion | flops 545259520 | bytes 6456320 | tf_op jit(solution)/shard_map/dot_general | solution.py:105
  182.3 0.7 copy.25
  183.1 5.7 %all-to-all-start.1 = ((bf16[16,16,128]{2,1,0:T(8,128)(2,1)}), bf16[16,16,128]{2,1,0:T(8,128)(2,1)S(1)}, u32[]{:S(2)}, u32[]{:S(2)}) async-start(bf16[16,16,128]{2,1,0:T(8,128)(2,1)} %bitcast.3), calls=%async_computation.1 | async-start | bytes 131072 | tf_op jit(solution)/shard_map/all_to_all | solution.py:121
  188.7 7.5 %fusion.3 = f32[256,512]{1,0:T(8,128)S(1)} fusion(bf16[8192,640]{1,0:T(8,128)(2,1)} %all-gather.6.cloned.1.call-done, bf16[256,8192]{1,0:T(8,128)(2,1)} %all-gather.4.cloned.1.call-done, f32[8192]{0:T(1024)S(1)} %convert_element_type.60, f32[256]{0:T(256)S(1)} %add_rsqrt_fusion.1), kind=kOutput, calls=%fused_computation.5 | convolution fusion | flops 2155872256 | bytes 13140992 | tf_op jit(solution)/shard_map/dot_general | solution.py:104
  197.3 0.8 convert_element_type.63
  198.1 5.7 %all-to-all-start = ((bf16[16,16,512]{2,1,0:T(8,128)(2,1)}), bf16[16,16,512]{2,1,0:T(8,128)(2,1)S(1)}, u32[]{:S(2)}, u32[]{:S(2)}) async-start(bf16[16,16,512]{2,1,0:T(8,128)(2,1)} %convert_element_type.63), calls=%async_computation | async-start | bytes 524288 | tf_op jit(solution)/shard_map/all_to_all | solution.py:120
  203.9 7.3 %all-to-all-done = bf16[16,16,512]{2,1,0:T(8,128)(2,1)S(1)} async-done(((bf16[16,16,512]{2,1,0:T(8,128)(2,1)}), bf16[16,16,512]{2,1,0:T(8,128)(2,1)S(1)}, u32[]{:S(2)}, u32[]{:S(2)}) %all-to-all-start) | async-done | bytes 262176 | tf_op jit(solution)/shard_map/all_to_all | solution.py:120
  211.8 6.2 %fusion.24 = (f32[16,8,8]{2,1,0:T(8,128)S(1)}, f32[16,8,8,192]{3,2,1,0:T(8,128)S(1)}) fusion(bf16[16,8,8,128]{3,2,1,0:T(8,128)(2,1)S(1)} %reshape.181, bf16[16,8,192,128]{3,2,1,0:T(8,128)(2,1)} %param.15, pred[16,192]{1,0:T(8,128)(4,1)S(1)} %iota_compare_fusion), kind=kOutput, calls=%fused_computation.50 | convolution fusion | flops 50920448 | bytes 7347200 | tf_op jit(solution)/shard_map/nkgd,nkld->nkgl/dot_general | solution.py:57
  218.5 4.6 %fusion.8 = bf16[16,8,8,128]{3,2,1,0:T(8,128)(2,1)S(1)} fusion(bf16[16,8,192,128]{3,2,1,0:T(8,128)(2,1)} %param.16, f32[16,8,8,192]{3,2,1,0:T(8,128)S(1)} %get-tuple-element.15, f32[16,8,8]{2,1,0:T(8,128)S(1)} %get-tuple-element.7, f32[16,8,8]{2,1,0:T(8,128)S(1)} %multiply_maximum_fusion, f32[16,8,128]{2,1,0:T(8,128)S(1)} %bitcast.37, ...), kind=kOutput, calls=%fused_computation.13 | convolution fusion | flops 51314688 | bytes 7417856 | tf_op jit(solution)/shard_map/nkgl,nkld->nkgd/dot_general | solution.py:72
  223.3 0.9 copy.27
  224.1 3.9 all-to-all-start.2
  228.0 58.9 %all-gather.8.cloned.1.call-done = bf16[512,8192]{1,0:T(8,128)(2,1)} async-done(((bf16[512,1024]{1,0:T(8,128)(2,1)}), bf16[512,8192]{1,0:T(8,128)(2,1)}) %all-gather.8.cloned.1.call-update) | async-done | bytes 8388624 | tf_op jit(solution)/shard_map/all_gather | solution.py:129
  287.0 9.0 %fusion.26 = f32[256,8192]{1,0:T(8,128)} fusion(bf16[256,512]{1,0:T(8,128)(2,1)S(1)} %bitcast.32, bf16[512,8192]{1,0:T(8,128)(2,1)} %all-gather.8.cloned.1.call-done), kind=kOutput, calls=%fused_computation.52 | convolution fusion | flops 2147483648 | bytes 17039360 | tf_op jit(solution)/shard_map/dot_general | solution.py:127
  295.9 95.3 %reduce-scatter.2.cloned.1.call-done = f32[256,512]{1,0:T(8,128)} async-done(((f32[256,8192]{1,0:T(8,128)}), f32[256,512]{1,0:T(8,128)}) %reduce-scatter.2.cloned.1.call-update) | async-done | bytes 524304 | tf_op jit(solution)/shard_map/reduce_scatter | solution.py:132
  391.3 1.2 multiply_reduce_fusion
  393.1 5.7 %all-to-all-start.3 = ((f32[16,1,256]{2,1,0:T(1,128)}), f32[16,1,256]{2,1,0:T(1,128)S(1)}, u32[]{:S(2)}, u32[]{:S(2)}) async-start(f32[16,1,256]{2,1,0:T(1,128)} %broadcast_in_dim.12), calls=%async_computation.4 | async-start | bytes 32768 | tf_op jit(solution)/shard_map/all_to_all | solution.py:21
  398.8 0.8 dynamic-slice_convert_fusion
  399.5 5.0 %all-to-all-done.3 = f32[16,1,256]{2,1,0:T(1,128)S(1)} async-done(((f32[16,1,256]{2,1,0:T(1,128)}), f32[16,1,256]{2,1,0:T(1,128)S(1)}, u32[]{:S(2)}, u32[]{:S(2)}) %all-to-all-start.3) | async-done | bytes 16416 | tf_op jit(solution)/shard_map/all_to_all | solution.py:21
  404.6 2.1 multiply_convert_fusion
  (37 shorter events, 6.9 us)
Async XLA Ops:
  7.2 43.2 %all-gather.4.cloned.1.call-start = ((), (), s32[]{:S(2)}) async-start(), calls=%async_computation.5 | async-start | bytes 4456448 | tf_op jit(solution)/shard_map/all_gather | solution.py:100
  7.9 169.5 %all-gather.6.cloned.1.call-start = ((), (), s32[]{:S(2)}) async-start(), calls=%async_computation.6 | async-start | bytes 11796480 | tf_op jit(solution)/shard_map/all_gather | solution.py:12
  10.5 276.5 %all-gather.8.cloned.1.call-start = ((), (), s32[]{:S(2)}) async-start(), calls=%async_computation.7 | async-start | bytes 9437184 | tf_op jit(solution)/shard_map/all_gather | solution.py:129
  183.1 15.0 %all-to-all-start.1 = ((bf16[16,16,128]{2,1,0:T(8,128)(2,1)}), bf16[16,16,128]{2,1,0:T(8,128)(2,1)S(1)}, u32[]{:S(2)}, u32[]{:S(2)}) async-start(bf16[16,16,128]{2,1,0:T(8,128)(2,1)} %bitcast.3), calls=%async_computation.1 | async-start | bytes 131072 | tf_op jit(solution)/shard_map/all_to_all | solution.py:121
  198.1 13.1 %all-to-all-start = ((bf16[16,16,512]{2,1,0:T(8,128)(2,1)}), bf16[16,16,512]{2,1,0:T(8,128)(2,1)S(1)}, u32[]{:S(2)}, u32[]{:S(2)}) async-start(bf16[16,16,512]{2,1,0:T(8,128)(2,1)} %convert_element_type.63), calls=%async_computation | async-start | bytes 524288 | tf_op jit(solution)/shard_map/all_to_all | solution.py:120
  224.1 62.9 %all-to-all-start.2 = ((bf16[16,16,512]{2,0,1:T(8,128)(2,1)}), bf16[16,16,512]{2,0,1:T(8,128)(2,1)S(1)}, u32[]{:S(2)}, u32[]{:S(2)}) async-start(bf16[16,16,512]{2,0,1:T(8,128)(2,1)} %copy.27), calls=%async_computation.2 | async-start | bytes 524288 | tf_op jit(solution)/shard_map/all_to_all | solution.py:126
  228.0 163.3 %reduce-scatter.2.cloned.1.call-start = ((), (), s32[]{:S(2)}) async-start(), calls=%async_computation.8 | async-start | bytes 8912896 | tf_op jit(solution)/shard_map/reduce_scatter | solution.py:132
  295.9 95.4 %copy-start = (bf16[256,512]{1,0:T(8,128)(2,1)S(1)}, bf16[256,512]{1,0:T(8,128)(2,1)}, u32[]{:S(2)}) copy-start(bf16[256,512]{1,0:T(8,128)(2,1)} %param.9) | copy-start | bytes 786436
  393.1 11.5 %all-to-all-start.3 = ((f32[16,1,256]{2,1,0:T(1,128)}), f32[16,1,256]{2,1,0:T(1,128)S(1)}, u32[]{:S(2)}, u32[]{:S(2)}) async-start(f32[16,1,256]{2,1,0:T(1,128)} %broadcast_in_dim.12), calls=%async_computation.4 | async-start | bytes 32768 | tf_op jit(solution)/shard_map/all_to_all | solution.py:21
Sparse Core Ops, SparseCore 0:
  9.6 40.6 all-gather.3
  52.6 124.6 all-gather.5
  179.7 107.2 all-gather.7
  296.1 95.1 reduce-scatter.1
where the time goes:
time: 414 us; the launch traced here: 413 us
  waiting for transfers between devices  328 us (79%)
  matrix products  32.1 us (8%)
  starting transfers between devices  21.2 us (5%)
  between operations  13.9 us (3%)
  other arithmetic  13.4 us (3%)
  local copies, waits for them, and re-layouts  4.48 us (1%)
    all_gather x1, waiting for transfers between devices, sent_together(): lax.all_gather(both, axis, axis=dim, tiled=True)  124 us
    reduce_scatter x1, waiting for transfers between devices, local(): lax.psum_scatter(partial_value, 'shard', scatter_dimension=1, tiled=True)  95.3 us
    all_gather x1, waiting for transfers between devices, local(): lax.all_gather(w_output, 'group', axis=1, tiled=True)  58.9 us
    all_gather x1, waiting for transfers between devices, local(): lax.all_gather(hidden_state, 'shard', axis=1, tiled=True)  36.4 us
    dot_general x1, matrix products, local(): jnp.dot(back_rows, lax.all_gather(w_output, 'group', axis=1, tiled=True),...  8.95 us
  transfers between devices with their start and end apart: 8, of which 6 were waited for; matrix products, arithmetic and copies ran while one was open for 9% of the time, Pallas kernels for 0%

commit v1 on v0

--- a/solution.py
+++ b/solution.py
@@ -1,10 +1,27 @@
+import functools
 import jax
 import jax.numpy as jnp
 from jax import lax
 from jax.sharding import PartitionSpec as P
+from jax.lax import all_to_all, axis_size
 
 epsilon = 1e-05
 rope_base = 500000.0
+
+
+def expand_threads(array_in, axis_name):
+    return jnp.concatenate(
+        all_to_all(
+            jnp.stack([array_in] * axis_size(axis_name), axis=0),
+            axis_name=axis_name,
+            split_axis=0,
+            concat_axis=0,
+        ),
+        axis=1,
+    )
+
+
+detail_indices_in = functools.partial(expand_threads, axis_name="group")
 
 
 def sent_together(arrays, axis, dim, along):
@@ -125,9 +142,7 @@
     context = attend(owner_q, owner_kv, cache_keys, cache_values, owner_len)
     back_rows = lax.all_to_all(context, "shard", split_axis=1, concat_axis=0, tiled=True)
     partial_value = jnp.dot(
-        back_rows,
-        lax.all_gather(w_output, "group", axis=1, tiled=True),
-        preferred_element_type=jnp.float32,
+        back_rows, detail_indices_in(w_output), preferred_element_type=jnp.float32
     )
     summed = lax.psum_scatter(partial_value, "shard", scatter_dimension=1, tiled=True)
     ffn_scale = lax.dynamic_slice_in_dim(ffn_gain.astype(jnp.float32), col_start, local_width)

time: 414 us -> 451 us (1.089)
  waiting for transfers between devices: 328 us -> 350 us
  blocking collectives: 0 us -> 11.1 us
    all_to_all x1, waiting for transfers between devices: 0.01 us -> 80.9 us  [expand_threads(): all_to_all(jnp.stack([array_in] * axis_size(axis_name), axis=0), axis_nam...]
    all_gather x1 -> x0, waiting for transfers between devices: 58.9 us -> none  [local(): lax.all_gather(w_output, 'group', axis=1, tiled=True)]
    all_to_all x0 -> x1, blocking collectives: none -> 11.1 us  [local(): lax.all_to_all(context, 'shard', split_axis=1, concat_axis=0, tiled=True)]
  transfers between devices with their start and end apart: 8 -> 7, of which waited for: 6 -> 6; matrix products, arithmetic and copies ran while one was open for 9% -> 7% of each run, Pallas kernels for 0% -> 0%
where the time goes in v1:
time: 451 us; the launch traced here: 450 us
  waiting for transfers between devices  350 us (78%)
  matrix products  31.9 us (7%)
  starting transfers between devices  22.1 us (5%)
  between operations  13.9 us (3%)
  other arithmetic  13.4 us (3%)
  blocking collectives  11.1 us (2%)
  local copies, waits for them, and re-layouts  7.6 us (2%)
    all_gather x1, waiting for transfers between devices, sent_together(): lax.all_gather(both, axis, axis=dim, tiled=True)  124 us
    reduce_scatter x1, waiting for transfers between devices, local(): lax.psum_scatter(partial_value, 'shard', scatter_dimension=1, tiled=True)  95 us
    all_to_all x1, waiting for transfers between devices, expand_threads(): all_to_all(jnp.stack([array_in] * axis_size(axis_name), axis=0), axis_nam...  80.9 us
    all_gather x1, waiting for transfers between devices, local(): lax.all_gather(hidden_state, 'shard', axis=1, tiled=True)  37.9 us
    all_to_all x1, blocking collectives, local(): lax.all_to_all(context, 'shard', split_axis=1, concat_axis=0, tiled=True)  11.1 us
    dot_general x1, matrix products, local(): jnp.dot(back_rows, detail_indices_in(w_output), preferred_element_type=jn...  9.11 us
  transfers between devices with their start and end apart: 7, of which 6 were waited for; matrix products, arithmetic and copies ran while one was open for 7% of the time, Pallas kernels for 0%

profile of v1, /device:TPU:1, one launch (start us, length us, event | category | flops | bytes accessed | tf_op | source)
XLA Modules:
  0.0 450.4 jit_solution(2764077932932250490)
XLA Ops:
  7.9 2.5 pad_maximum_fusion
  12.5 37.9 %all-gather.3.cloned.1.call-done = bf16[256,8192]{1,0:T(8,128)(2,1)} async-done(((bf16[256,512]{1,0:T(8,128)(2,1)}), bf16[256,8192]{1,0:T(8,128)(2,1)}) %all-gather.3.cloned.1.call-update) | async-done | bytes 4194320 | tf_op jit(solution)/shard_map/all_gather | solution.py:117
  50.3 3.1 fusion
  53.5 123.9 %all-gather.5.cloned.1.call-done = bf16[8192,640]{1,0:T(8,128)(2,1)} async-done(((bf16[1024,640]{1,0:T(8,128)(2,1)}), bf16[8192,640]{1,0:T(8,128)(2,1)}) %all-gather.5.cloned.1.call-update) | async-done | bytes 10485776 | tf_op jit(solution)/shard_map/all_gather | solution.py:29
  177.4 4.6 %fusion.5 = f32[256,128]{0,1:T(8,128)S(1)} fusion(bf16[8192,640]{1,0:T(8,128)(2,1)} %all-gather.5.cloned.1.call-done, bf16[256,8192]{1,0:T(8,128)(2,1)} %all-gather.3.cloned.1.call-done, f32[8192]{0:T(1024)S(1)} %convert_element_type.60, f32[256]{0:T(256)S(1)} %add_rsqrt_fusion.1), kind=kOutput, calls=%fused_computation.7 | convolution fusion | flops 545259520 | bytes 6456320 | tf_op jit(solution)/shard_map/dot_general | solution.py:122
  182.3 0.7 copy.28
  183.1 5.7 %all-to-all-start.1 = ((bf16[16,16,128]{2,1,0:T(8,128)(2,1)}), bf16[16,16,128]{2,1,0:T(8,128)(2,1)S(1)}, u32[]{:S(2)}, u32[]{:S(2)}) async-start(bf16[16,16,128]{2,1,0:T(8,128)(2,1)} %bitcast.3), calls=%async_computation.1 | async-start | bytes 131072 | tf_op jit(solution)/shard_map/all_to_all | solution.py:138
  188.8 7.1 %fusion.3 = f32[256,512]{1,0:T(8,128)S(1)} fusion(bf16[8192,640]{1,0:T(8,128)(2,1)} %all-gather.5.cloned.1.call-done, bf16[256,8192]{1,0:T(8,128)(2,1)} %all-gather.3.cloned.1.call-done, f32[8192]{0:T(1024)S(1)} %convert_element_type.60, f32[256]{0:T(256)S(1)} %add_rsqrt_fusion.1), kind=kOutput, calls=%fused_computation.5 | convolution fusion | flops 2155872256 | bytes 13140992 | tf_op jit(solution)/shard_map/dot_general | solution.py:121
  196.9 0.8 convert_element_type.63
  197.7 5.7 %all-to-all-start = ((bf16[16,16,512]{2,1,0:T(8,128)(2,1)}), bf16[16,16,512]{2,1,0:T(8,128)(2,1)S(1)}, u32[]{:S(2)}, u32[]{:S(2)}) async-start(bf16[16,16,512]{2,1,0:T(8,128)(2,1)} %convert_element_type.63), calls=%async_computation | async-start | bytes 524288 | tf_op jit(solution)/shard_map/all_to_all | solution.py:137
  204.0 6.8 %all-to-all-done = bf16[16,16,512]{2,1,0:T(8,128)(2,1)S(1)} async-done(((bf16[16,16,512]{2,1,0:T(8,128)(2,1)}), bf16[16,16,512]{2,1,0:T(8,128)(2,1)S(1)}, u32[]{:S(2)}, u32[]{:S(2)}) %all-to-all-start) | async-done | bytes 262176 | tf_op jit(solution)/shard_map/all_to_all | solution.py:137
  210.8 4.0 stack.2
  214.7 5.1 %all-to-all-start.3 = ((bf16[8,512,1024]{1,2,0:T(8,128)(2,1)}), bf16[8,512,1024]{1,2,0:T(8,128)(2,1)}, u32[]{:S(2)}, u32[]{:S(2)}) async-start(bf16[8,512,1024]{1,2,0:T(8,128)(2,1)} %stack.2), calls=%async_computation.3 | async-start | bytes 16777216 | tf_op jit(solution)/shard_map/all_to_all | solution.py:14
  220.9 6.2 %fusion.24 = (f32[16,8,8]{2,1,0:T(8,128)S(1)}, f32[16,8,8,192]{3,2,1,0:T(8,128)S(1)}) fusion(bf16[16,8,8,128]{3,2,1,0:T(8,128)(2,1)S(1)} %reshape.189, bf16[16,8,192,128]{3,2,1,0:T(8,128)(2,1)} %param.15, pred[16,192]{1,0:T(8,128)(4,1)S(1)} %iota_compare_fusion), kind=kOutput, calls=%fused_computation.50 | convolution fusion | flops 50920448 | bytes 7347200 | tf_op jit(solution)/shard_map/nkgd,nkld->nkgl/dot_general | solution.py:74
  227.6 4.6 %fusion.8 = bf16[16,8,8,128]{3,2,1,0:T(8,128)(2,1)S(1)} fusion(bf16[16,8,192,128]{3,2,1,0:T(8,128)(2,1)} %param.16, f32[16,8,8,192]{3,2,1,0:T(8,128)S(1)} %get-tuple-element.15, f32[16,8,8]{2,1,0:T(8,128)S(1)} %get-tuple-element.7, f32[16,8,8]{2,1,0:T(8,128)S(1)} %multiply_maximum_fusion, f32[16,8,128]{2,1,0:T(8,128)S(1)} %bitcast.40, ...), kind=kOutput, calls=%fused_computation.13 | convolution fusion | flops 51314688 | bytes 7417856 | tf_op jit(solution)/shard_map/nkgl,nkld->nkgd/dot_general | solution.py:89
  232.6 80.9 %all-to-all-done.3 = bf16[8,512,1024]{1,2,0:T(8,128)(2,1)} async-done(((bf16[8,512,1024]{1,2,0:T(8,128)(2,1)}), bf16[8,512,1024]{1,2,0:T(8,128)(2,1)}, u32[]{:S(2)}, u32[]{:S(2)}) %all-to-all-start.3) | async-done | bytes 8388640 | tf_op jit(solution)/shard_map/all_to_all | solution.py:14
  313.4 11.1 %all_to_all.59 = bf16[16,16,512]{2,0,1:T(8,128)(2,1)S(1)} all-to-all(bf16[16,16,512]{2,0,1:T(8,128)(2,1)S(1)} %copy.30), channel_id=1, replica_groups=mesh['group'=8,'shard'=16] {'shard'}, dimensions={1} | all-to-all | bytes 524288 | tf_op jit(solution)/shard_map/all_to_all | solution.py:143
  324.6 9.1 %fusion.26 = f32[256,8192]{1,0:T(8,128)} fusion(bf16[256,512]{1,0:T(8,128)(2,1)S(1)} %bitcast.35, bf16[512,8192]{0,1:T(8,128)(2,1)} %bitcast.10), kind=kOutput, calls=%fused_computation.52 | convolution fusion | flops 2147483648 | bytes 17039360 | tf_op jit(solution)/shard_map/dot_general | solution.py:144
  333.7 95.0 %reduce-scatter.2.cloned.1.call-done = f32[256,512]{1,0:T(8,128)} async-done(((f32[256,8192]{1,0:T(8,128)}), f32[256,512]{1,0:T(8,128)}) %reduce-scatter.2.cloned.1.call-update) | async-done | bytes 524304 | tf_op jit(solution)/shard_map/reduce_scatter | solution.py:147
  428.7 1.2 multiply_reduce_fusion
  430.5 5.4 %all-to-all-start.4 = ((f32[16,1,256]{2,1,0:T(1,128)}), f32[16,1,256]{2,1,0:T(1,128)S(1)}, u32[]{:S(2)}, u32[]{:S(2)}) async-start(f32[16,1,256]{2,1,0:T(1,128)} %broadcast_in_dim.12), calls=%async_computation.5 | async-start | bytes 32768 | tf_op jit(solution)/shard_map/all_to_all | solution.py:38
  435.9 0.8 dynamic-slice_convert_fusion
  436.7 5.0 %all-to-all-done.4 = f32[16,1,256]{2,1,0:T(1,128)S(1)} async-done(((f32[16,1,256]{2,1,0:T(1,128)}), f32[16,1,256]{2,1,0:T(1,128)S(1)}, u32[]{:S(2)}, u32[]{:S(2)}) %all-to-all-start.4) | async-done | bytes 16416 | tf_op jit(solution)/shard_map/all_to_all | solution.py:38
  441.7 2.1 multiply_convert_fusion
  (41 shorter events, 7.1 us)
Async XLA Ops:
  7.2 43.2 %all-gather.3.cloned.1.call-start = ((), (), s32[]{:S(2)}) async-start(), calls=%async_computation.6 | async-start | bytes 4456448 | tf_op jit(solution)/shard_map/all_gather | solution.py:117
  7.9 169.5 %all-gather.5.cloned.1.call-start = ((), (), s32[]{:S(2)}) async-start(), calls=%async_computation.7 | async-start | bytes 11796480 | tf_op jit(solution)/shard_map/all_gather | solution.py:29
  183.1 14.7 %all-to-all-start.1 = ((bf16[16,16,128]{2,1,0:T(8,128)(2,1)}), bf16[16,16,128]{2,1,0:T(8,128)(2,1)S(1)}, u32[]{:S(2)}, u32[]{:S(2)}) async-start(bf16[16,16,128]{2,1,0:T(8,128)(2,1)} %bitcast.3), calls=%async_computation.1 | async-start | bytes 131072 | tf_op jit(solution)/shard_map/all_to_all | solution.py:138
  188.7 14.7 %copy-start.1 = (bf16[512,1024]{1,0:T(8,128)(2,1)S(1)}, bf16[512,1024]{1,0:T(8,128)(2,1)}, u32[]{:S(2)}) copy-start(bf16[512,1024]{1,0:T(8,128)(2,1)} %param.14) | copy-start | bytes 3145732
  197.7 13.1 %all-to-all-start = ((bf16[16,16,512]{2,1,0:T(8,128)(2,1)}), bf16[16,16,512]{2,1,0:T(8,128)(2,1)S(1)}, u32[]{:S(2)}, u32[]{:S(2)}) async-start(bf16[16,16,512]{2,1,0:T(8,128)(2,1)} %convert_element_type.63), calls=%async_computation | async-start | bytes 524288 | tf_op jit(solution)/shard_map/all_to_all | solution.py:137
  214.7 5.3 %copy-start.2 = (s32[256]{0:T(256)S(1)}, s32[256]{0:T(256)}, u32[]{:S(2)}) copy-start(s32[256]{0:T(256)} %param.17) | copy-start | bytes 3076
  214.7 98.7 %all-to-all-start.3 = ((bf16[8,512,1024]{1,2,0:T(8,128)(2,1)}), bf16[8,512,1024]{1,2,0:T(8,128)(2,1)}, u32[]{:S(2)}, u32[]{:S(2)}) async-start(bf16[8,512,1024]{1,2,0:T(8,128)(2,1)} %stack.2), calls=%async_computation.3 | async-start | bytes 16777216 | tf_op jit(solution)/shard_map/all_to_all | solution.py:14
  219.8 208.9 %reduce-scatter.2.cloned.1.call-start = ((), (), s32[]{:S(2)}) async-start(), calls=%async_computation.8 | async-start | bytes 8912896 | tf_op jit(solution)/shard_map/reduce_scatter | solution.py:147
  333.7 95.1 %copy-start = (bf16[256,512]{1,0:T(8,128)(2,1)S(1)}, bf16[256,512]{1,0:T(8,128)(2,1)}, u32[]{:S(2)}) copy-start(bf16[256,512]{1,0:T(8,128)(2,1)} %param.9) | copy-start | bytes 786436
  430.5 11.2 %all-to-all-start.4 = ((f32[16,1,256]{2,1,0:T(1,128)}), f32[16,1,256]{2,1,0:T(1,128)S(1)}, u32[]{:S(2)}, u32[]{:S(2)}) async-start(f32[16,1,256]{2,1,0:T(1,128)} %broadcast_in_dim.12), calls=%async_computation.5 | async-start | bytes 32768 | tf_op jit(solution)/shard_map/all_to_all | solution.py:38
Sparse Core Ops, SparseCore 0:
  9.6 40.6 all-gather.2
  52.6 124.6 all-gather.4
  333.8 94.8 reduce-scatter.1
